TPU v7x, 32 devices: a whole 2x2x4 slice. The times are simulated.
32 devices in a mesh: layer: 8 (over z, x), split: 4 (over y, core).
Axes of the slice: x: 2, y: 2, z: 4, core: 2. Of those that a mesh axis runs over, the one named last changes fastest.
Arguments:
- right_side: float32 [32, 512, 128], P('layer', 'split'), may hold values from -6 to 6
- diagonal: float32 [32, 512, 128], P('layer', 'split'), may hold values from 0.1 to 1
- inverses: float32 [32, 512, 512], P('layer', None, 'split'), may hold values from -1 to 1, as said below
Outputs:
- solution_field: float32 [32, 512, 128], P('layer', 'split')
- residual: float32 [32, 512, 128], P('layer', 'split')
Inputs may be any that keep to these rules, and one draw needn't show every extreme that they name: `inverses`: each plane's inverse is a diagonal matrix with entries between 0.5 and 1 plus a dense coupling with zero diagonal and spectral norm below 0.2.
All inputs are finite; a program needn't handle non-finite values.
Results may differ from a plain program's by a relative error of at most 0.0003.
Values sent between devices are 32-bit elements; how exact they have to be, the bound alone decides.
No kernel may reach another device: no remote copies, remote signals or barrier semaphores. Data moves between devices by JAX's collectives and lax.ppermute only.
A program may use at most 64 MiB of HBM per device.

v0:
```python
import jax
import jax.numpy as jnp
from jax import lax
from jax.sharding import PartitionSpec as P


def with_halo(x, sides, width):
    for axis, dim in sides:
        size, length = (lax.axis_size(axis), x.shape[dim])
        up = [(i, (i + 1) % size) for i in range(size - 1)]
        down = [(j, i) for i, j in up]
        last = lax.slice_in_dim(x, length - width, length, axis=dim)
        first = lax.slice_in_dim(x, 0, width, axis=dim)
        before = lax.ppermute(last, axis, up)
        after = lax.ppermute(first, axis, down)
        x = jnp.concatenate([before, x, after], axis=dim)
    return x


def from_behind(block, axis, distance):
    devices = range(lax.axis_size(axis))
    route = [(i - distance, i) for i in devices if i - distance in devices]
    return lax.ppermute(block, axis, route)


def stencil(values, diagonal):
    padded = with_halo(values, (("layer", 0), ("split", 1)), 1)
    beside = padded[2:, 1:-1, :] + padded[:-2, 1:-1, :]
    beside = beside + padded[1:-1, 2:, :] + padded[1:-1, :-2, :]
    centre_part = padded[1:-1, 1:-1, :]
    y_upper = jnp.pad(centre_part[:, :, 1:], ((0, 0), (0, 0), (0, 1)))
    y_lower = jnp.pad(centre_part[:, :, :-1], ((0, 0), (0, 0), (1, 0)))
    return (6.0 + diagonal) * values - beside - y_upper - y_lower


def down_local(matrices, portion, carried):

    def down_advance(state, inputs):
        matrix, source = inputs
        state = jnp.dot(matrix, source + state, precision=lax.Precision.HIGHEST)
        return (state, state)

    return lax.scan(down_advance, carried, (matrices, portion))


def up_local(matrices, portion, carried):

    def up_advance(state, inputs):
        matrix, below = inputs
        state = below + jnp.dot(matrix, state, precision=lax.Precision.HIGHEST)
        return (state, state)

    return lax.scan(up_advance, carried, (matrices, portion), reverse=True)


def chain_sweep(sweep_fn, matrices, source, sender, anchor, nblocks):
    depth_count = lax.axis_size("layer")
    block_width = source.shape[2] // nblocks
    plane_shape = (source.shape[1], block_width)
    result = jnp.zeros_like(source)
    incoming = jnp.zeros(plane_shape, jnp.float32)

    def chain_advance(turn, state):
        result, incoming = state
        block_raw = turn - anchor
        active = jnp.logical_and(block_raw >= 0, block_raw < nblocks)

        def working(unused):
            return sweep_fn(matrices, source, incoming)

        def resting(unused):
            return (jnp.zeros(plane_shape, jnp.float32), jnp.zeros_like(source))

        outgoing, stacked = lax.cond(active, working, resting, None)
        previous = result
        result = jnp.where(active, stacked, previous)
        return (result, sender(outgoing))

    result, incoming = lax.fori_loop(
        0, depth_count + nblocks - 1, chain_advance, (result, incoming)
    )
    return result


def per_device(right_side, diagonal, inverses):
    matrices = lax.all_gather(inverses, "split", axis=2, tiled=True)
    columns = lax.all_to_all(right_side, "split", split_axis=2, concat_axis=1, tiled=True)
    nblocks = 1
    own_index = lax.axis_index("layer")
    depth_count = lax.axis_size("layer")
    applied_rhs = stencil(right_side, diagonal)

    def send_down(values):
        return from_behind(values, "layer", 1)

    def send_up(values):
        return from_behind(values, "layer", -1)

    lower_sweep = chain_sweep(down_local, matrices, columns, send_down, own_index, nblocks)
    upper_sweep = chain_sweep(
        up_local, matrices, lower_sweep, send_up, depth_count - 1 - own_index, nblocks
    )
    direction = lax.all_to_all(upper_sweep, "split", split_axis=1, concat_axis=2, tiled=True)
    image = stencil(direction, diagonal)
    applied_image = stencil(image, diagonal)
    sums_all = lax.psum(
        (
            jnp.sum(right_side * right_side),
            jnp.sum(right_side * image),
            jnp.sum(applied_rhs * right_side),
            jnp.sum(applied_rhs * image),
            jnp.sum(applied_image * right_side),
            jnp.sum(applied_image * image),
            jnp.sum(applied_rhs * applied_rhs),
            jnp.sum(applied_rhs * applied_image),
            jnp.sum(applied_image * applied_image),
        ),
        ("layer", "split"),
    )
    (
        norm_sq,
        curv_sum,
        rhs_rhs,
        rhs_image,
        image_rhs,
        image_image,
        arhs_arhs,
        arhs_aimage,
        aimage_aimage,
    ) = sums_all
    step_alpha = norm_sq / curv_sum
    middle = right_side - step_alpha * image
    tangent = applied_rhs - step_alpha * applied_image
    cross_sum = (
        rhs_rhs - step_alpha * (rhs_image + image_rhs) + step_alpha * step_alpha * image_image
    )
    self_sum = arhs_arhs - 2.0 * step_alpha * arhs_aimage + step_alpha * step_alpha * aimage_aimage
    step_omega = cross_sum / self_sum
    solution_field = step_alpha * direction + step_omega * middle
    residual = middle - step_omega * tangent
    return (solution_field, residual)


def solution(mesh):
    placed = (P("layer", "split", None), P("layer", "split", None), P("layer", None, "split"))
    return jax.shard_map(
        per_device,
        mesh=mesh,
        in_specs=placed,
        out_specs=(P("layer", "split", None), P("layer", "split", None)),
        check_vma=False,
    )
```

profile of v0, /device:TPU:12, one launch (start us, length us, event | category | flops | bytes accessed | tf_op | source)
XLA Modules:
  0.0 438.9 jit_solution(2182941142321325081)
XLA Ops:
  9.7 3.9 all-to-all-start
  23.4 21.4 %all-gather.2.cloned.1.call-done = f32[4,512,512]{2,1,0:T(8,128)} async-done(((f32[4,512,128]{2,1,0:T(8,128)}), f32[4,512,512]{2,1,0:T(8,128)}) %all-gather.2.cloned.1.call-update) | async-done | bytes 4194320 | tf_op jit(solution)/shard_map/all_gather | solution.py:86
  44.8 112.2 %while.60 = (s32[]{:T(128)}, f32[4,512,32]{1,2,0:T(8,128)S(1)}, f32[512,32]{0,1:T(8,128)S(1)}, s32[]{:T(128)}, f32[4,512,512]{2,1,0:T(8,128)}, /*index=5*/f32[4,512,32]{1,2,0:T(8,128)S(1)}, s32[]{:T(128)}, s32[]{:T(128)}) while((s32[]{:T(128)}, f32[4,512,32]{1,2,0:T(8,128)S(1)}, f32[512,32]{0,1:T(8,128)S(1)}, s32[]{:T(128)}, ...), condition=%wide.region_7.8_spmd.clone, body=%wide.region_2.7_spmd.clone.sunk | while | flops 100810760 | bytes 2623315 | solution.py:79
  45.5 3.4 collective-permute-start.1
  49.0 3.6 collective-permute-done.1
  55.9 22.0 %collective-permute-done.1 = f32[512,32]{0,1:T(8,128)S(1)} collective-permute-done((f32[512,32]{0,1:T(8,128)S(1)}, f32[512,32]{0,1:T(8,128)S(1)}, u32[]{:S(2)}, u32[]{:S(2)}) %collective-permute-start.1) | collective-permute-done | bytes 65568 | tf_op jit(solution)/shard_map/while/body/eval_jaxpr/ppermute | solution.py:23
  77.9 11.7 %conditional.6 = (f32[512,32]{0,1:T(8,128)S(1)}, f32[4,512,32]{1,2,0:T(8,128)}) conditional(s32[]{:T(128)} %convert_element_type.26, () %tuple.150, (f32[4,512,512]{2,1,0:T(8,128)}, f32[4,512,32]{1,2,0:T(8,128)S(1)}, f32[512,32]{0,1:T(8,128)S(1)}) %tuple.151), branch_computations={%region_3.3_spmd, %region_4.6_spmd} | conditional | flops 100679680 | bytes 1574541 | solution.py:74
  77.9 11.7 %while.58 = (s32[]{:T(128)}, f32[512,32]{0,1:T(8,128)S(1)}, f32[4,512,32]{1,2,0:T(8,128)}, f32[4,512,512]{2,1,0:T(8,128)}, f32[4,512,32]{1,2,0:T(8,128)S(1)}, /*index=5*/s32[]{:T(128)}) while((s32[]{:T(128)}, f32[512,32]{0,1:T(8,128)S(1)}, f32[4,512,32]{1,2,0:T(8,128)}, f32[4,512,512]{2,1,0:T(8,128)}, f32[4,512,32]{1,2,0:T(8,128)S(1)}, ...), condition=%wide.region_6.5_spmd, body=%wide.region_5.4_spmd.sunk | while | flops 100679680 | bytes 1443397 | solution.py:43
  92.6 4.1 collective-permute-done.1
  97.4 12.0 %collective-permute-start.1 = (f32[512,32]{0,1:T(8,128)S(1)}, f32[512,32]{0,1:T(8,128)S(1)}, u32[]{:S(2)}, u32[]{:S(2)}) collective-permute-start(f32[512,32]{0,1:T(8,128)S(1)} %get-tuple-element.643), channel_id=1, source_target_pairs={{0,4},{4,8},{8,12},{12,16},{16,20},{20,24},{24,28},{1,5},{5,9},{9,... | collective-permute-start | bytes 196616 | tf_op jit(solution)/shard_map/while/body/eval_jaxpr/ppermute | solution.py:23
  112.0 4.3 collective-permute-start.1
  119.8 12.9 %collective-permute-start.1 = (f32[512,32]{0,1:T(8,128)S(1)}, f32[512,32]{0,1:T(8,128)S(1)}, u32[]{:S(2)}, u32[]{:S(2)}) collective-permute-start(f32[512,32]{0,1:T(8,128)S(1)} %get-tuple-element.643), channel_id=1, source_target_pairs={{0,4},{4,8},{8,12},{12,16},{16,20},{20,24},{24,28},{1,5},{5,9},{9,... | collective-permute-start | bytes 196616 | tf_op jit(solution)/shard_map/while/body/eval_jaxpr/ppermute | solution.py:23
  135.3 5.2 %collective-permute-start.1 = (f32[512,32]{0,1:T(8,128)S(1)}, f32[512,32]{0,1:T(8,128)S(1)}, u32[]{:S(2)}, u32[]{:S(2)}) collective-permute-start(f32[512,32]{0,1:T(8,128)S(1)} %get-tuple-element.643), channel_id=1, source_target_pairs={{0,4},{4,8},{8,12},{12,16},{16,20},{20,24},{24,28},{1,5},{5,9},{9,... | collective-permute-start | bytes 196616 | tf_op jit(solution)/shard_map/while/body/eval_jaxpr/ppermute | solution.py:23
  143.1 12.0 %collective-permute-start.1 = (f32[512,32]{0,1:T(8,128)S(1)}, f32[512,32]{0,1:T(8,128)S(1)}, u32[]{:S(2)}, u32[]{:S(2)}) collective-permute-start(f32[512,32]{0,1:T(8,128)S(1)} %get-tuple-element.643), channel_id=1, source_target_pairs={{0,4},{4,8},{8,12},{12,16},{16,20},{20,24},{24,28},{1,5},{5,9},{9,... | collective-permute-start | bytes 196616 | tf_op jit(solution)/shard_map/while/body/eval_jaxpr/ppermute | solution.py:23
  157.0 155.7 %while.61 = (s32[]{:T(128)}, f32[4,512,32]{1,2,0:T(8,128)S(1)}, f32[512,32]{0,1:T(8,128)S(1)}, s32[]{:T(128)}, f32[4,512,32]{1,2,0:T(8,128)S(1)}, /*index=5*/f32[4,512,512]{2,1,0:T(8,128)}, s32[]{:T(128)}, s32[]{:T(128)}) while((s32[]{:T(128)}, f32[4,512,32]{1,2,0:T(8,128)S(1)}, f32[512,32]{0,1:T(8,128)S(1)}, s32[]{:T(128)}, ...), condition=%wide.region_13.14_spmd.clone, body=%wide.region_8.13_spmd.clone.sunk | while | flops 100810760 | bytes 2884979 | solution.py:79
  159.8 5.4 %collective-permute-done = f32[512,32]{0,1:T(8,128)S(1)} collective-permute-done((f32[512,32]{0,1:T(8,128)S(1)}, f32[512,32]{0,1:T(8,128)S(1)}, u32[]{:S(2)}, u32[]{:S(2)}) %collective-permute-start) | collective-permute-done | bytes 65568 | tf_op jit(solution)/shard_map/while/body/eval_jaxpr/ppermute | solution.py:23
  168.2 13.4 %collective-permute-done = f32[512,32]{0,1:T(8,128)S(1)} collective-permute-done((f32[512,32]{0,1:T(8,128)S(1)}, f32[512,32]{0,1:T(8,128)S(1)}, u32[]{:S(2)}, u32[]{:S(2)}) %collective-permute-start) | collective-permute-done | bytes 65568 | tf_op jit(solution)/shard_map/while/body/eval_jaxpr/ppermute | solution.py:23
  184.4 5.0 %collective-permute-done = f32[512,32]{0,1:T(8,128)S(1)} collective-permute-done((f32[512,32]{0,1:T(8,128)S(1)}, f32[512,32]{0,1:T(8,128)S(1)}, u32[]{:S(2)}, u32[]{:S(2)}) %collective-permute-start) | collective-permute-done | bytes 65568 | tf_op jit(solution)/shard_map/while/body/eval_jaxpr/ppermute | solution.py:23
  192.2 11.9 %collective-permute-done = f32[512,32]{0,1:T(8,128)S(1)} collective-permute-done((f32[512,32]{0,1:T(8,128)S(1)}, f32[512,32]{0,1:T(8,128)S(1)}, u32[]{:S(2)}, u32[]{:S(2)}) %collective-permute-start) | collective-permute-done | bytes 65568 | tf_op jit(solution)/shard_map/while/body/eval_jaxpr/ppermute | solution.py:23
  206.9 62.3 %collective-permute-done = f32[512,32]{0,1:T(8,128)S(1)} collective-permute-done((f32[512,32]{0,1:T(8,128)S(1)}, f32[512,32]{0,1:T(8,128)S(1)}, u32[]{:S(2)}, u32[]{:S(2)}) %collective-permute-start) | collective-permute-done | bytes 65568 | tf_op jit(solution)/shard_map/while/body/eval_jaxpr/ppermute | solution.py:23
  269.2 12.4 %conditional.7 = (f32[512,32]{0,1:T(8,128)S(1)}, f32[4,512,32]{1,2,0:T(8,128)}) conditional(s32[]{:T(128)} %convert_element_type.27, () %tuple.153, (f32[4,512,32]{1,2,0:T(8,128)S(1)}, f32[4,512,512]{2,1,0:T(8,128)}, f32[512,32]{0,1:T(8,128)S(1)}) %tuple.154), branch_computations={%region_9.9_spmd, %region_10.12_spmd} | conditional | flops 100679680 | bytes 1836205 | solution.py:74
  270.0 11.7 %while.59 = (s32[]{:T(128)}, f32[512,32]{0,1:T(8,128)S(1)}, f32[4,512,32]{1,2,0:T(8,128)}, f32[4,512,32]{1,2,0:T(8,128)S(1)}, f32[4,512,512]{2,1,0:T(8,128)}, /*index=5*/s32[]{:T(128)}, s32[]{:T(128)}) while((s32[]{:T(128)}, f32[512,32]{0,1:T(8,128)S(1)}, f32[4,512,32]{1,2,0:T(8,128)}, f32[4,512,32]{1,2,0:T(8,128)S(1)}, ...), condition=%wide.region_12.11_spmd, body=%wide.region_11.10_spmd.sunk | while | flops 100679680 | bytes 1442905 | solution.py:53
  288.5 14.5 %collective-permute-start = (f32[512,32]{0,1:T(8,128)S(1)}, f32[512,32]{0,1:T(8,128)S(1)}, u32[]{:S(2)}, u32[]{:S(2)}) collective-permute-start(f32[512,32]{0,1:T(8,128)S(1)} %get-tuple-element.651), channel_id=1, source_target_pairs={{4,0},{8,4},{12,8},{16,12},{20,16},{24,20},{28,24},{5,1},{9,5},{13... | collective-permute-start | bytes 196616 | tf_op jit(solution)/shard_map/while/body/eval_jaxpr/ppermute | solution.py:23
  305.7 5.2 %collective-permute-start = (f32[512,32]{0,1:T(8,128)S(1)}, f32[512,32]{0,1:T(8,128)S(1)}, u32[]{:S(2)}, u32[]{:S(2)}) collective-permute-start(f32[512,32]{0,1:T(8,128)S(1)} %get-tuple-element.651), channel_id=1, source_target_pairs={{4,0},{8,4},{12,8},{16,12},{20,16},{24,20},{28,24},{5,1},{9,5},{13... | collective-permute-start | bytes 196616 | tf_op jit(solution)/shard_map/while/body/eval_jaxpr/ppermute | solution.py:23
  314.5 5.1 %all-to-all-start.1 = ((f32[4,1,16384]{2,1,0:T(1,128)}), f32[4,1,16384]{2,1,0:T(1,128)S(1)}, u32[]{:S(2)}, u32[]{:S(2)}) async-start(f32[4,1,16384]{2,1,0:T(1,128)} %reshape.6), calls=%async_computation.1 | async-start | bytes 524288 | tf_op jit(solution)/shard_map/all_to_all | solution.py:103
  319.6 4.3 all-to-all-done.1
  326.8 12.7 %collective-permute-start.2 = (f32[1,128,128]{1,2,0:T(8,128)S(1)}, f32[1,128,128]{1,2,0:T(8,128)S(1)}, u32[]{:S(2)}, u32[]{:S(2)}) collective-permute-start(f32[1,128,128]{1,2,0:T(8,128)S(1)} %bitcast.60), channel_id=1, source_target_pairs={{4,0},{8,4},{12,8},{16,12},{20,16},{24,20},{28,24},{5,1},{9,5},{13... | collective-permute-start | bytes 196616 | tf_op jit(solution)/shard_map/ppermute | solution.py:15
  341.8 4.7 %collective-permute-done.3 = f32[1,128,128]{1,2,0:T(8,128)S(1)} collective-permute-done((f32[1,128,128]{1,2,0:T(8,128)S(1)}, f32[1,128,128]{1,2,0:T(8,128)S(1)}, u32[]{:S(2)}, u32[]{:S(2)}) %collective-permute-start.3) | collective-permute-done | bytes 65568 | tf_op jit(solution)/shard_map/ppermute | solution.py:14
  354.0 3.8 collective-permute-done.5
  358.1 3.4 collective-permute-start.10
  377.2 3.8 collective-permute-done.13
  383.4 41.7 %all-reduce.6 = (f32[]{:T(128)}, f32[]{:T(128)}, f32[]{:T(128)}, f32[]{:T(128)}, f32[]{:T(128)}, /*index=5*/f32[]{:T(128)}, f32[]{:T(128)}, f32[]{:T(128)}) all-reduce(f32[]{:T(128)} %get-tuple-element.434, f32[]{:T(128)} %multiply_reduce_fusion.8, f32[]{:T(128)} %get-tuple-element.433, ...), channel_id=1, replica_groups=mesh['layer'=8,'split'=4] {'layer','split'}, use_global_device_ids=true, to_apply=%region_17.18 | all-reduce | flops 8 | bytes 64 | tf_op jit(solution)/shard_map/psum | solution.py:106
  (152 shorter events, 126.2 us)
Async XLA Ops:
  7.2 37.6 %all-gather.2.cloned.1.call-start = ((), (), s32[]{:S(2)}) async-start(), calls=%async_computation.2 | async-start | bytes 5242880 | tf_op jit(solution)/shard_map/all_gather | solution.py:86
  9.7 13.7 %all-to-all-start = ((f32[4,128,128]{1,0,2:T(4,128)}), f32[4,128,128]{1,0,2:T(4,128)S(1)}, u32[]{:S(2)}, u32[]{:S(2)}) async-start(f32[4,128,128]{1,0,2:T(4,128)} %copy.44), calls=%async_computation | async-start | bytes 524288 | tf_op jit(solution)/shard_map/all_to_all | solution.py:87
  14.7 326.8 %collective-permute-start.6 = (f32[1,128,128]{1,2,0:T(8,128)S(1)}, f32[1,128,128]{1,2,0:T(8,128)S(1)}, u32[]{:S(2)}, u32[]{:S(2)}) collective-permute-start(f32[1,128,128]{1,2,0:T(8,128)S(1)} %get-tuple-element.507), channel_id=1, source_target_pairs={{4,0},{8,4},{12,8},{16,12},{20,16},{24,20},{28,24},{5,1},{9,5},{13... | collective-permute-start | bytes 196616 | tf_op jit(solution)/shard_map/ppermute | solution.py:15
  18.0 323.5 %collective-permute-start.7 = (f32[1,128,128]{1,2,0:T(8,128)S(1)}, f32[1,128,128]{1,2,0:T(8,128)S(1)}, u32[]{:S(2)}, u32[]{:S(2)}) collective-permute-start(f32[1,128,128]{1,2,0:T(8,128)S(1)} %get-tuple-element.506), channel_id=1, source_target_pairs={{0,4},{4,8},{8,12},{12,16},{16,20},{20,24},{24,28},{1,5},{5,9},{9,... | collective-permute-start | bytes 196616 | tf_op jit(solution)/shard_map/ppermute | solution.py:14
  45.5 7.0 %collective-permute-start.1 = (f32[512,32]{0,1:T(8,128)S(1)}, f32[512,32]{0,1:T(8,128)S(1)}, u32[]{:S(2)}, u32[]{:S(2)}) collective-permute-start(f32[512,32]{0,1:T(8,128)S(1)} %get-tuple-element.643), channel_id=1, source_target_pairs={{0,4},{4,8},{8,12},{12,16},{16,20},{20,24},{24,28},{1,5},{5,9},{9,... | collective-permute-start | bytes 196616 | tf_op jit(solution)/shard_map/while/body/eval_jaxpr/ppermute | solution.py:23
  53.3 24.6 %collective-permute-start.1 = (f32[512,32]{0,1:T(8,128)S(1)}, f32[512,32]{0,1:T(8,128)S(1)}, u32[]{:S(2)}, u32[]{:S(2)}) collective-permute-start(f32[512,32]{0,1:T(8,128)S(1)} %get-tuple-element.643), channel_id=1, source_target_pairs={{0,4},{4,8},{8,12},{12,16},{16,20},{20,24},{24,28},{1,5},{5,9},{9,... | collective-permute-start | bytes 196616 | tf_op jit(solution)/shard_map/while/body/eval_jaxpr/ppermute | solution.py:23
  89.6 7.1 %collective-permute-start.1 = (f32[512,32]{0,1:T(8,128)S(1)}, f32[512,32]{0,1:T(8,128)S(1)}, u32[]{:S(2)}, u32[]{:S(2)}) collective-permute-start(f32[512,32]{0,1:T(8,128)S(1)} %get-tuple-element.643), channel_id=1, source_target_pairs={{0,4},{4,8},{8,12},{12,16},{16,20},{20,24},{24,28},{1,5},{5,9},{9,... | collective-permute-start | bytes 196616 | tf_op jit(solution)/shard_map/while/body/eval_jaxpr/ppermute | solution.py:23
  97.4 13.9 %collective-permute-start.1 = (f32[512,32]{0,1:T(8,128)S(1)}, f32[512,32]{0,1:T(8,128)S(1)}, u32[]{:S(2)}, u32[]{:S(2)}) collective-permute-start(f32[512,32]{0,1:T(8,128)S(1)} %get-tuple-element.643), channel_id=1, source_target_pairs={{0,4},{4,8},{8,12},{12,16},{16,20},{20,24},{24,28},{1,5},{5,9},{9,... | collective-permute-start | bytes 196616 | tf_op jit(solution)/shard_map/while/body/eval_jaxpr/ppermute | solution.py:23
  112.0 7.0 %collective-permute-start.1 = (f32[512,32]{0,1:T(8,128)S(1)}, f32[512,32]{0,1:T(8,128)S(1)}, u32[]{:S(2)}, u32[]{:S(2)}) collective-permute-start(f32[512,32]{0,1:T(8,128)S(1)} %get-tuple-element.643), channel_id=1, source_target_pairs={{0,4},{4,8},{8,12},{12,16},{16,20},{20,24},{24,28},{1,5},{5,9},{9,... | collective-permute-start | bytes 196616 | tf_op jit(solution)/shard_map/while/body/eval_jaxpr/ppermute | solution.py:23
  119.8 14.8 %collective-permute-start.1 = (f32[512,32]{0,1:T(8,128)S(1)}, f32[512,32]{0,1:T(8,128)S(1)}, u32[]{:S(2)}, u32[]{:S(2)}) collective-permute-start(f32[512,32]{0,1:T(8,128)S(1)} %get-tuple-element.643), channel_id=1, source_target_pairs={{0,4},{4,8},{8,12},{12,16},{16,20},{20,24},{24,28},{1,5},{5,9},{9,... | collective-permute-start | bytes 196616 | tf_op jit(solution)/shard_map/while/body/eval_jaxpr/ppermute | solution.py:23
  135.3 7.0 %collective-permute-start.1 = (f32[512,32]{0,1:T(8,128)S(1)}, f32[512,32]{0,1:T(8,128)S(1)}, u32[]{:S(2)}, u32[]{:S(2)}) collective-permute-start(f32[512,32]{0,1:T(8,128)S(1)} %get-tuple-element.643), channel_id=1, source_target_pairs={{0,4},{4,8},{8,12},{12,16},{16,20},{20,24},{24,28},{1,5},{5,9},{9,... | collective-permute-start | bytes 196616 | tf_op jit(solution)/shard_map/while/body/eval_jaxpr/ppermute | solution.py:23
  143.1 13.9 %collective-permute-start.1 = (f32[512,32]{0,1:T(8,128)S(1)}, f32[512,32]{0,1:T(8,128)S(1)}, u32[]{:S(2)}, u32[]{:S(2)}) collective-permute-start(f32[512,32]{0,1:T(8,128)S(1)} %get-tuple-element.643), channel_id=1, source_target_pairs={{0,4},{4,8},{8,12},{12,16},{16,20},{20,24},{24,28},{1,5},{5,9},{9,... | collective-permute-start | bytes 196616 | tf_op jit(solution)/shard_map/while/body/eval_jaxpr/ppermute | solution.py:23
  157.7 7.4 %collective-permute-start = (f32[512,32]{0,1:T(8,128)S(1)}, f32[512,32]{0,1:T(8,128)S(1)}, u32[]{:S(2)}, u32[]{:S(2)}) collective-permute-start(f32[512,32]{0,1:T(8,128)S(1)} %get-tuple-element.651), channel_id=1, source_target_pairs={{4,0},{8,4},{12,8},{16,12},{20,16},{24,20},{28,24},{5,1},{9,5},{13... | collective-permute-start | bytes 196616 | tf_op jit(solution)/shard_map/while/body/eval_jaxpr/ppermute | solution.py:23
  165.9 15.7 %collective-permute-start = (f32[512,32]{0,1:T(8,128)S(1)}, f32[512,32]{0,1:T(8,128)S(1)}, u32[]{:S(2)}, u32[]{:S(2)}) collective-permute-start(f32[512,32]{0,1:T(8,128)S(1)} %get-tuple-element.651), channel_id=1, source_target_pairs={{4,0},{8,4},{12,8},{16,12},{20,16},{24,20},{28,24},{5,1},{9,5},{13... | collective-permute-start | bytes 196616 | tf_op jit(solution)/shard_map/while/body/eval_jaxpr/ppermute | solution.py:23
  182.4 7.0 %collective-permute-start = (f32[512,32]{0,1:T(8,128)S(1)}, f32[512,32]{0,1:T(8,128)S(1)}, u32[]{:S(2)}, u32[]{:S(2)}) collective-permute-start(f32[512,32]{0,1:T(8,128)S(1)} %get-tuple-element.651), channel_id=1, source_target_pairs={{4,0},{8,4},{12,8},{16,12},{20,16},{24,20},{28,24},{5,1},{9,5},{13... | collective-permute-start | bytes 196616 | tf_op jit(solution)/shard_map/while/body/eval_jaxpr/ppermute | solution.py:23
  190.1 14.0 %collective-permute-start = (f32[512,32]{0,1:T(8,128)S(1)}, f32[512,32]{0,1:T(8,128)S(1)}, u32[]{:S(2)}, u32[]{:S(2)}) collective-permute-start(f32[512,32]{0,1:T(8,128)S(1)} %get-tuple-element.651), channel_id=1, source_target_pairs={{4,0},{8,4},{12,8},{16,12},{20,16},{24,20},{28,24},{5,1},{9,5},{13... | collective-permute-start | bytes 196616 | tf_op jit(solution)/shard_map/while/body/eval_jaxpr/ppermute | solution.py:23
  204.8 64.4 %collective-permute-start = (f32[512,32]{0,1:T(8,128)S(1)}, f32[512,32]{0,1:T(8,128)S(1)}, u32[]{:S(2)}, u32[]{:S(2)}) collective-permute-start(f32[512,32]{0,1:T(8,128)S(1)} %get-tuple-element.651), channel_id=1, source_target_pairs={{4,0},{8,4},{12,8},{16,12},{20,16},{24,20},{28,24},{5,1},{9,5},{13... | collective-permute-start | bytes 196616 | tf_op jit(solution)/shard_map/while/body/eval_jaxpr/ppermute | solution.py:23
  281.7 6.2 %collective-permute-start = (f32[512,32]{0,1:T(8,128)S(1)}, f32[512,32]{0,1:T(8,128)S(1)}, u32[]{:S(2)}, u32[]{:S(2)}) collective-permute-start(f32[512,32]{0,1:T(8,128)S(1)} %get-tuple-element.651), channel_id=1, source_target_pairs={{4,0},{8,4},{12,8},{16,12},{20,16},{24,20},{28,24},{5,1},{9,5},{13... | collective-permute-start | bytes 196616 | tf_op jit(solution)/shard_map/while/body/eval_jaxpr/ppermute | solution.py:23
  288.5 16.4 %collective-permute-start = (f32[512,32]{0,1:T(8,128)S(1)}, f32[512,32]{0,1:T(8,128)S(1)}, u32[]{:S(2)}, u32[]{:S(2)}) collective-permute-start(f32[512,32]{0,1:T(8,128)S(1)} %get-tuple-element.651), channel_id=1, source_target_pairs={{4,0},{8,4},{12,8},{16,12},{20,16},{24,20},{28,24},{5,1},{9,5},{13... | collective-permute-start | bytes 196616 | tf_op jit(solution)/shard_map/while/body/eval_jaxpr/ppermute | solution.py:23
  305.7 7.0 %collective-permute-start = (f32[512,32]{0,1:T(8,128)S(1)}, f32[512,32]{0,1:T(8,128)S(1)}, u32[]{:S(2)}, u32[]{:S(2)}) collective-permute-start(f32[512,32]{0,1:T(8,128)S(1)} %get-tuple-element.651), channel_id=1, source_target_pairs={{4,0},{8,4},{12,8},{16,12},{20,16},{24,20},{28,24},{5,1},{9,5},{13... | collective-permute-start | bytes 196616 | tf_op jit(solution)/shard_map/while/body/eval_jaxpr/ppermute | solution.py:23
  314.5 9.4 %all-to-all-start.1 = ((f32[4,1,16384]{2,1,0:T(1,128)}), f32[4,1,16384]{2,1,0:T(1,128)S(1)}, u32[]{:S(2)}, u32[]{:S(2)}) async-start(f32[4,1,16384]{2,1,0:T(1,128)} %reshape.6), calls=%async_computation.1 | async-start | bytes 524288 | tf_op jit(solution)/shard_map/all_to_all | solution.py:103
  326.8 15.1 %collective-permute-start.2 = (f32[1,128,128]{1,2,0:T(8,128)S(1)}, f32[1,128,128]{1,2,0:T(8,128)S(1)}, u32[]{:S(2)}, u32[]{:S(2)}) collective-permute-start(f32[1,128,128]{1,2,0:T(8,128)S(1)} %bitcast.60), channel_id=1, source_target_pairs={{4,0},{8,4},{12,8},{16,12},{20,16},{24,20},{28,24},{5,1},{9,5},{13... | collective-permute-start | bytes 196616 | tf_op jit(solution)/shard_map/ppermute | solution.py:15
  339.5 7.1 %collective-permute-start.3 = (f32[1,128,128]{1,2,0:T(8,128)S(1)}, f32[1,128,128]{1,2,0:T(8,128)S(1)}, u32[]{:S(2)}, u32[]{:S(2)}) collective-permute-start(f32[1,128,128]{1,2,0:T(8,128)S(1)} %bitcast.61), channel_id=1, source_target_pairs={{0,4},{4,8},{8,12},{12,16},{16,20},{20,24},{24,28},{1,5},{5,9},{9,... | collective-permute-start | bytes 196616 | tf_op jit(solution)/shard_map/ppermute | solution.py:14
  346.8 7.2 %collective-permute-start.4 = (f32[6,1,128]{1,2,0:T(8,128)S(1)}, f32[6,1,128]{1,2,0:T(8,128)S(1)}, u32[]{:S(2)}, u32[]{:S(2)}) collective-permute-start(f32[6,1,128]{1,2,0:T(8,128)S(1)} %get-tuple-element.500), channel_id=1, source_target_pairs={{1,0},{2,1},{3,2},{5,4},{6,5},{7,6},{9,8},{10,9},{11,10},{13,12},{... | collective-permute-start | bytes 9224 | tf_op jit(solution)/shard_map/ppermute | solution.py:15
  348.7 9.1 %collective-permute-start.5 = (f32[6,1,128]{1,2,0:T(8,128)S(1)}, f32[6,1,128]{1,2,0:T(8,128)S(1)}, u32[]{:S(2)}, u32[]{:S(2)}) collective-permute-start(f32[6,1,128]{1,2,0:T(8,128)S(1)} %get-tuple-element.501), channel_id=1, source_target_pairs={{0,1},{1,2},{2,3},{4,5},{5,6},{6,7},{8,9},{9,10},{10,11},{12,13},{... | collective-permute-start | bytes 9224 | tf_op jit(solution)/shard_map/ppermute | solution.py:14
  358.1 10.4 %collective-permute-start.10 = (f32[1,128,128]{1,2,0:T(8,128)S(1)}, f32[1,128,128]{1,2,0:T(8,128)S(1)}, u32[]{:S(2)}, u32[]{:S(2)}) collective-permute-start(f32[1,128,128]{1,2,0:T(8,128)S(1)} %get-tuple-element.503), channel_id=1, source_target_pairs={{4,0},{8,4},{12,8},{16,12},{20,16},{24,20},{28,24},{5,1},{9,5},{13... | collective-permute-start | bytes 196616 | tf_op jit(solution)/shard_map/ppermute | solution.py:15
  361.5 7.1 %collective-permute-start.11 = (f32[1,128,128]{1,2,0:T(8,128)S(1)}, f32[1,128,128]{1,2,0:T(8,128)S(1)}, u32[]{:S(2)}, u32[]{:S(2)}) collective-permute-start(f32[1,128,128]{1,2,0:T(8,128)S(1)} %get-tuple-element.502), channel_id=1, source_target_pairs={{0,4},{4,8},{8,12},{12,16},{16,20},{20,24},{24,28},{1,5},{5,9},{9,... | collective-permute-start | bytes 196616 | tf_op jit(solution)/shard_map/ppermute | solution.py:14
  364.1 9.7 %collective-permute-start.8 = (f32[6,1,128]{1,2,0:T(8,128)S(1)}, f32[6,1,128]{1,2,0:T(8,128)S(1)}, u32[]{:S(2)}, u32[]{:S(2)}) collective-permute-start(f32[6,1,128]{1,2,0:T(8,128)S(1)} %get-tuple-element.498), channel_id=1, source_target_pairs={{1,0},{2,1},{3,2},{5,4},{6,5},{7,6},{9,8},{10,9},{11,10},{13,12},{... | collective-permute-start | bytes 9224 | tf_op jit(solution)/shard_map/ppermute | solution.py:15
  366.1 9.1 %collective-permute-start.9 = (f32[6,1,128]{1,2,0:T(8,128)S(1)}, f32[6,1,128]{1,2,0:T(8,128)S(1)}, u32[]{:S(2)}, u32[]{:S(2)}) collective-permute-start(f32[6,1,128]{1,2,0:T(8,128)S(1)} %get-tuple-element.499), channel_id=1, source_target_pairs={{0,1},{1,2},{2,3},{4,5},{5,6},{6,7},{8,9},{9,10},{10,11},{12,13},{... | collective-permute-start | bytes 9224 | tf_op jit(solution)/shard_map/ppermute | solution.py:14
  368.8 8.4 %collective-permute-start.12 = (f32[6,1,128]{1,2,0:T(8,128)S(1)}, f32[6,1,128]{1,2,0:T(8,128)S(1)}, u32[]{:S(2)}, u32[]{:S(2)}) collective-permute-start(f32[6,1,128]{1,2,0:T(8,128)S(1)} %get-tuple-element.496), channel_id=1, source_target_pairs={{1,0},{2,1},{3,2},{5,4},{6,5},{7,6},{9,8},{10,9},{11,10},{13,12},{... | collective-permute-start | bytes 9224 | tf_op jit(solution)/shard_map/ppermute | solution.py:15
  371.9 9.1 %collective-permute-start.13 = (f32[6,1,128]{1,2,0:T(8,128)S(1)}, f32[6,1,128]{1,2,0:T(8,128)S(1)}, u32[]{:S(2)}, u32[]{:S(2)}) collective-permute-start(f32[6,1,128]{1,2,0:T(8,128)S(1)} %get-tuple-element.497), channel_id=1, source_target_pairs={{0,1},{1,2},{2,3},{4,5},{5,6},{6,7},{8,9},{9,10},{10,11},{12,13},{... | collective-permute-start | bytes 9224 | tf_op jit(solution)/shard_map/ppermute | solution.py:14
Sparse Core Ops, SparseCore 0:
  9.5 35.1 all-gather.1
where the time goes:
time: 441 us; the launch traced here: 439 us
  waiting for transfers between devices  189 us (43%)
  starting transfers between devices  134 us (30%)
  blocking collectives  41.7 us (9%)
  matrix products  23.3 us (5%)
  local copies, waits for them, and re-layouts  20.9 us (5%)
  between operations  20.8 us (5%)
  other arithmetic  8.15 us (2%)
    ppermute x16, waiting for transfers between devices, from_behind(): return lax.ppermute(block, axis, route)  144 us
    ppermute x16, starting transfers between devices, from_behind(): return lax.ppermute(block, axis, route)  85.4 us
    psum x1, blocking collectives, per_device(): lax.psum((jnp.sum(right_side * right_side), jnp.sum(right_side * image),...  41.7 us
    ppermute x6, starting transfers between devices, with_halo(): after = lax.ppermute(first, axis, down)  26.3 us
    all_gather x1, waiting for transfers between devices, per_device(): matrices = lax.all_gather(inverses, 'split', axis=2, tiled=True)  21.4 us
    ppermute x6, starting transfers between devices, with_halo(): before = lax.ppermute(last, axis, up)  13.7 us
    ppermute x6, waiting for transfers between devices, with_halo(): before = lax.ppermute(last, axis, up)  13.7 us
    dot_general x4, matrix products, down_advance(): state = jnp.dot(matrix, source + state, precision=lax.Precision.HIGHEST)  11.7 us
  transfers between devices with their start and end apart: 31, of which 24 were waited for; matrix products, arithmetic and copies ran while one was open for 11% of the time, Pallas kernels for 0%

commit v1 on v0

--- a/solution.py
+++ b/solution.py
@@ -103,20 +103,19 @@
     direction = lax.all_to_all(upper_sweep, "split", split_axis=1, concat_axis=2, tiled=True)
     image = stencil(direction, diagonal)
     applied_image = stencil(image, diagonal)
-    sums_all = lax.psum(
-        (
-            jnp.sum(right_side * right_side),
-            jnp.sum(right_side * image),
-            jnp.sum(applied_rhs * right_side),
-            jnp.sum(applied_rhs * image),
-            jnp.sum(applied_image * right_side),
-            jnp.sum(applied_image * image),
-            jnp.sum(applied_rhs * applied_rhs),
-            jnp.sum(applied_rhs * applied_image),
-            jnp.sum(applied_image * applied_image),
-        ),
-        ("layer", "split"),
+    sums_all = (
+        jnp.sum(right_side * right_side),
+        jnp.sum(right_side * image),
+        jnp.sum(applied_rhs * right_side),
+        jnp.sum(applied_rhs * image),
+        jnp.sum(applied_image * right_side),
+        jnp.sum(applied_image * image),
+        jnp.sum(applied_rhs * applied_rhs),
+        jnp.sum(applied_rhs * applied_image),
+        jnp.sum(applied_image * applied_image),
     )
+    for i0 in ("layer", "split"):
+        sums_all = lax.psum(sums_all, axis_name=i0)
     (
         norm_sq,
         curv_sum,

time: 441 us -> 426 us (0.966)
  blocking collectives: 41.7 us -> 24 us
    psum x1 -> x2, blocking collectives: 41.7 us -> 24 us  [per_device(): sums_all = lax.psum(sums_all, axis_name=i0)]
  transfers between devices with their start and end apart: 31 -> 31, of which waited for: 24 -> 24; matrix products, arithmetic and copies ran while one was open for 11% -> 12% of each run, Pallas kernels for 0% -> 0%
where the time goes in v1:
time: 426 us; the launch traced here: 421 us
  waiting for transfers between devices  189 us (44%)
  starting transfers between devices  134 us (31%)
  blocking collectives  24 us (6%)
  matrix products  23.3 us (5%)
  local copies, waits for them, and re-layouts  20.9 us (5%)
  between operations  20.7 us (5%)
  other arithmetic  8.09 us (2%)
    ppermute x16, waiting for transfers between devices, from_behind(): return lax.ppermute(block, axis, route)  144 us
    ppermute x16, starting transfers between devices, from_behind(): return lax.ppermute(block, axis, route)  85.4 us
    ppermute x6, starting transfers between devices, with_halo(): after = lax.ppermute(first, axis, down)  26.3 us
    psum x2, blocking collectives, per_device(): sums_all = lax.psum(sums_all, axis_name=i0)  24 us
    all_gather x1, waiting for transfers between devices, per_device(): matrices = lax.all_gather(inverses, 'split', axis=2, tiled=True)  21.4 us
    ppermute x6, starting transfers between devices, with_halo(): before = lax.ppermute(last, axis, up)  13.7 us
    ppermute x6, waiting for transfers between devices, with_halo(): before = lax.ppermute(last, axis, up)  13.7 us
    dot_general x4, matrix products, down_advance(): state = jnp.dot(matrix, source + state, precision=lax.Precision.HIGHEST)  11.7 us
  transfers between devices with their start and end apart: 31, of which 24 were waited for; matrix products, arithmetic and copies ran while one was open for 12% of the time, Pallas kernels for 0%

profile of v1, /device:TPU:12, one launch (start us, length us, event | category | flops | bytes accessed | tf_op | source)
XLA Modules:
  0.0 421.2 jit_solution(10306473538622307949)
XLA Ops:
  9.7 3.9 all-to-all-start
  23.3 21.4 %all-gather.2.cloned.1.call-done = f32[4,512,512]{2,1,0:T(8,128)} async-done(((f32[4,512,128]{2,1,0:T(8,128)}), f32[4,512,512]{2,1,0:T(8,128)}) %all-gather.2.cloned.1.call-update) | async-done | bytes 4194320 | tf_op jit(solution)/shard_map/all_gather | solution.py:86
  44.8 112.2 %while.60 = (s32[]{:T(128)}, f32[4,512,32]{1,2,0:T(8,128)S(1)}, f32[512,32]{0,1:T(8,128)S(1)}, s32[]{:T(128)}, f32[4,512,512]{2,1,0:T(8,128)}, /*index=5*/f32[4,512,32]{1,2,0:T(8,128)S(1)}, s32[]{:T(128)}, s32[]{:T(128)}) while((s32[]{:T(128)}, f32[4,512,32]{1,2,0:T(8,128)S(1)}, f32[512,32]{0,1:T(8,128)S(1)}, s32[]{:T(128)}, ...), condition=%wide.region_8.9_spmd.clone, body=%wide.region_3.8_spmd.clone.sunk | while | flops 100810760 | bytes 2623315 | solution.py:79
  49.0 3.6 collective-permute-done.1
  55.9 22.0 %collective-permute-done.1 = f32[512,32]{0,1:T(8,128)S(1)} collective-permute-done((f32[512,32]{0,1:T(8,128)S(1)}, f32[512,32]{0,1:T(8,128)S(1)}, u32[]{:S(2)}, u32[]{:S(2)}) %collective-permute-start.1) | collective-permute-done | bytes 65568 | tf_op jit(solution)/shard_map/while/body/eval_jaxpr/ppermute | solution.py:23
  77.9 11.7 %conditional.6 = (f32[512,32]{0,1:T(8,128)S(1)}, f32[4,512,32]{1,2,0:T(8,128)}) conditional(s32[]{:T(128)} %convert_element_type.26, () %tuple.150, (f32[4,512,512]{2,1,0:T(8,128)}, f32[4,512,32]{1,2,0:T(8,128)S(1)}, f32[512,32]{0,1:T(8,128)S(1)}) %tuple.151), branch_computations={%region_4.4_spmd, %region_5.7_spmd} | conditional | flops 100679680 | bytes 1574541 | solution.py:74
  77.9 11.7 %while.58 = (s32[]{:T(128)}, f32[512,32]{0,1:T(8,128)S(1)}, f32[4,512,32]{1,2,0:T(8,128)}, f32[4,512,512]{2,1,0:T(8,128)}, f32[4,512,32]{1,2,0:T(8,128)S(1)}, /*index=5*/s32[]{:T(128)}) while((s32[]{:T(128)}, f32[512,32]{0,1:T(8,128)S(1)}, f32[4,512,32]{1,2,0:T(8,128)}, f32[4,512,512]{2,1,0:T(8,128)}, f32[4,512,32]{1,2,0:T(8,128)S(1)}, ...), condition=%wide.region_7.6_spmd, body=%wide.region_6.5_spmd.sunk | while | flops 100679680 | bytes 1443397 | solution.py:43
  92.6 4.1 collective-permute-done.1
  97.4 12.0 %collective-permute-start.1 = (f32[512,32]{0,1:T(8,128)S(1)}, f32[512,32]{0,1:T(8,128)S(1)}, u32[]{:S(2)}, u32[]{:S(2)}) collective-permute-start(f32[512,32]{0,1:T(8,128)S(1)} %get-tuple-element.651), channel_id=1, source_target_pairs={{0,4},{4,8},{8,12},{12,16},{16,20},{20,24},{24,28},{1,5},{5,9},{9,... | collective-permute-start | bytes 196616 | tf_op jit(solution)/shard_map/while/body/eval_jaxpr/ppermute | solution.py:23
  112.0 4.3 %collective-permute-start.1 = (f32[512,32]{0,1:T(8,128)S(1)}, f32[512,32]{0,1:T(8,128)S(1)}, u32[]{:S(2)}, u32[]{:S(2)}) collective-permute-start(f32[512,32]{0,1:T(8,128)S(1)} %get-tuple-element.651), channel_id=1, source_target_pairs={{0,4},{4,8},{8,12},{12,16},{16,20},{20,24},{24,28},{1,5},{5,9},{9,... | collective-permute-start | bytes 196616 | tf_op jit(solution)/shard_map/while/body/eval_jaxpr/ppermute | solution.py:23
  119.8 12.9 %collective-permute-start.1 = (f32[512,32]{0,1:T(8,128)S(1)}, f32[512,32]{0,1:T(8,128)S(1)}, u32[]{:S(2)}, u32[]{:S(2)}) collective-permute-start(f32[512,32]{0,1:T(8,128)S(1)} %get-tuple-element.651), channel_id=1, source_target_pairs={{0,4},{4,8},{8,12},{12,16},{16,20},{20,24},{24,28},{1,5},{5,9},{9,... | collective-permute-start | bytes 196616 | tf_op jit(solution)/shard_map/while/body/eval_jaxpr/ppermute | solution.py:23
  135.3 5.2 %collective-permute-start.1 = (f32[512,32]{0,1:T(8,128)S(1)}, f32[512,32]{0,1:T(8,128)S(1)}, u32[]{:S(2)}, u32[]{:S(2)}) collective-permute-start(f32[512,32]{0,1:T(8,128)S(1)} %get-tuple-element.651), channel_id=1, source_target_pairs={{0,4},{4,8},{8,12},{12,16},{16,20},{20,24},{24,28},{1,5},{5,9},{9,... | collective-permute-start | bytes 196616 | tf_op jit(solution)/shard_map/while/body/eval_jaxpr/ppermute | solution.py:23
  143.1 12.0 %collective-permute-start.1 = (f32[512,32]{0,1:T(8,128)S(1)}, f32[512,32]{0,1:T(8,128)S(1)}, u32[]{:S(2)}, u32[]{:S(2)}) collective-permute-start(f32[512,32]{0,1:T(8,128)S(1)} %get-tuple-element.651), channel_id=1, source_target_pairs={{0,4},{4,8},{8,12},{12,16},{16,20},{20,24},{24,28},{1,5},{5,9},{9,... | collective-permute-start | bytes 196616 | tf_op jit(solution)/shard_map/while/body/eval_jaxpr/ppermute | solution.py:23
  157.0 155.7 %while.61 = (s32[]{:T(128)}, f32[4,512,32]{1,2,0:T(8,128)S(1)}, f32[512,32]{0,1:T(8,128)S(1)}, s32[]{:T(128)}, f32[4,512,32]{1,2,0:T(8,128)S(1)}, /*index=5*/f32[4,512,512]{2,1,0:T(8,128)}, s32[]{:T(128)}, s32[]{:T(128)}) while((s32[]{:T(128)}, f32[4,512,32]{1,2,0:T(8,128)S(1)}, f32[512,32]{0,1:T(8,128)S(1)}, s32[]{:T(128)}, ...), condition=%wide.region_14.15_spmd.clone, body=%wide.region_9.0_spmd.clone.sunk | while | flops 100810760 | bytes 2884979 | solution.py:79
  159.8 5.4 %collective-permute-done = f32[512,32]{0,1:T(8,128)S(1)} collective-permute-done((f32[512,32]{0,1:T(8,128)S(1)}, f32[512,32]{0,1:T(8,128)S(1)}, u32[]{:S(2)}, u32[]{:S(2)}) %collective-permute-start) | collective-permute-done | bytes 65568 | tf_op jit(solution)/shard_map/while/body/eval_jaxpr/ppermute | solution.py:23
  168.2 13.4 %collective-permute-done = f32[512,32]{0,1:T(8,128)S(1)} collective-permute-done((f32[512,32]{0,1:T(8,128)S(1)}, f32[512,32]{0,1:T(8,128)S(1)}, u32[]{:S(2)}, u32[]{:S(2)}) %collective-permute-start) | collective-permute-done | bytes 65568 | tf_op jit(solution)/shard_map/while/body/eval_jaxpr/ppermute | solution.py:23
  184.4 5.0 %collective-permute-done = f32[512,32]{0,1:T(8,128)S(1)} collective-permute-done((f32[512,32]{0,1:T(8,128)S(1)}, f32[512,32]{0,1:T(8,128)S(1)}, u32[]{:S(2)}, u32[]{:S(2)}) %collective-permute-start) | collective-permute-done | bytes 65568 | tf_op jit(solution)/shard_map/while/body/eval_jaxpr/ppermute | solution.py:23
  192.2 11.9 %collective-permute-done = f32[512,32]{0,1:T(8,128)S(1)} collective-permute-done((f32[512,32]{0,1:T(8,128)S(1)}, f32[512,32]{0,1:T(8,128)S(1)}, u32[]{:S(2)}, u32[]{:S(2)}) %collective-permute-start) | collective-permute-done | bytes 65568 | tf_op jit(solution)/shard_map/while/body/eval_jaxpr/ppermute | solution.py:23
  206.9 62.3 %collective-permute-done = f32[512,32]{0,1:T(8,128)S(1)} collective-permute-done((f32[512,32]{0,1:T(8,128)S(1)}, f32[512,32]{0,1:T(8,128)S(1)}, u32[]{:S(2)}, u32[]{:S(2)}) %collective-permute-start) | collective-permute-done | bytes 65568 | tf_op jit(solution)/shard_map/while/body/eval_jaxpr/ppermute | solution.py:23
  269.2 12.4 %conditional.7 = (f32[512,32]{0,1:T(8,128)S(1)}, f32[4,512,32]{1,2,0:T(8,128)}) conditional(s32[]{:T(128)} %convert_element_type.27, () %tuple.153, (f32[4,512,32]{1,2,0:T(8,128)S(1)}, f32[4,512,512]{2,1,0:T(8,128)}, f32[512,32]{0,1:T(8,128)S(1)}) %tuple.154), branch_computations={%region_10.10_spmd, %region_11.13_spmd} | conditional | flops 100679680 | bytes 1836205 | solution.py:74
  270.0 11.7 %while.59 = (s32[]{:T(128)}, f32[512,32]{0,1:T(8,128)S(1)}, f32[4,512,32]{1,2,0:T(8,128)}, f32[4,512,32]{1,2,0:T(8,128)S(1)}, f32[4,512,512]{2,1,0:T(8,128)}, /*index=5*/s32[]{:T(128)}, s32[]{:T(128)}) while((s32[]{:T(128)}, f32[512,32]{0,1:T(8,128)S(1)}, f32[4,512,32]{1,2,0:T(8,128)}, f32[4,512,32]{1,2,0:T(8,128)S(1)}, ...), condition=%wide.region_13.12_spmd, body=%wide.region_12.11_spmd.sunk | while | flops 100679680 | bytes 1442905 | solution.py:53
  288.5 14.5 %collective-permute-start = (f32[512,32]{0,1:T(8,128)S(1)}, f32[512,32]{0,1:T(8,128)S(1)}, u32[]{:S(2)}, u32[]{:S(2)}) collective-permute-start(f32[512,32]{0,1:T(8,128)S(1)} %get-tuple-element.659), channel_id=1, source_target_pairs={{4,0},{8,4},{12,8},{16,12},{20,16},{24,20},{28,24},{5,1},{9,5},{13... | collective-permute-start | bytes 196616 | tf_op jit(solution)/shard_map/while/body/eval_jaxpr/ppermute | solution.py:23
  305.7 5.2 %collective-permute-start = (f32[512,32]{0,1:T(8,128)S(1)}, f32[512,32]{0,1:T(8,128)S(1)}, u32[]{:S(2)}, u32[]{:S(2)}) collective-permute-start(f32[512,32]{0,1:T(8,128)S(1)} %get-tuple-element.659), channel_id=1, source_target_pairs={{4,0},{8,4},{12,8},{16,12},{20,16},{24,20},{28,24},{5,1},{9,5},{13... | collective-permute-start | bytes 196616 | tf_op jit(solution)/shard_map/while/body/eval_jaxpr/ppermute | solution.py:23
  314.5 5.1 %all-to-all-start.1 = ((f32[4,1,16384]{2,1,0:T(1,128)}), f32[4,1,16384]{2,1,0:T(1,128)S(1)}, u32[]{:S(2)}, u32[]{:S(2)}) async-start(f32[4,1,16384]{2,1,0:T(1,128)} %reshape.6), calls=%async_computation.1 | async-start | bytes 524288 | tf_op jit(solution)/shard_map/all_to_all | solution.py:103
  319.6 4.3 %all-to-all-done.1 = f32[4,1,16384]{2,1,0:T(1,128)S(1)} async-done(((f32[4,1,16384]{2,1,0:T(1,128)}), f32[4,1,16384]{2,1,0:T(1,128)S(1)}, u32[]{:S(2)}, u32[]{:S(2)}) %all-to-all-start.1) | async-done | bytes 262176 | tf_op jit(solution)/shard_map/all_to_all | solution.py:103
  326.8 12.7 %collective-permute-start.2 = (f32[1,128,128]{1,2,0:T(8,128)S(1)}, f32[1,128,128]{1,2,0:T(8,128)S(1)}, u32[]{:S(2)}, u32[]{:S(2)}) collective-permute-start(f32[1,128,128]{1,2,0:T(8,128)S(1)} %bitcast.60), channel_id=1, source_target_pairs={{4,0},{8,4},{12,8},{16,12},{20,16},{24,20},{28,24},{5,1},{9,5},{13... | collective-permute-start | bytes 196616 | tf_op jit(solution)/shard_map/ppermute | solution.py:15
  341.8 4.7 %collective-permute-done.3 = f32[1,128,128]{1,2,0:T(8,128)S(1)} collective-permute-done((f32[1,128,128]{1,2,0:T(8,128)S(1)}, f32[1,128,128]{1,2,0:T(8,128)S(1)}, u32[]{:S(2)}, u32[]{:S(2)}) %collective-permute-start.3) | collective-permute-done | bytes 65568 | tf_op jit(solution)/shard_map/ppermute | solution.py:14
  354.0 3.8 collective-permute-done.5
  358.1 3.4 collective-permute-start.10
  377.2 3.8 collective-permute-done.13
  383.5 17.5 %all-reduce.6 = (f32[]{:T(128)}, f32[]{:T(128)}, f32[]{:T(128)}, f32[]{:T(128)}, f32[]{:T(128)}, /*index=5*/f32[]{:T(128)}, f32[]{:T(128)}, f32[]{:T(128)}) all-reduce(f32[]{:T(128)} %get-tuple-element.434, f32[]{:T(128)} %multiply_reduce_fusion.8, f32[]{:T(128)} %get-tuple-element.433, ...), channel_id=1, replica_groups=mesh['layer'=8,'split'=4] {'layer'}, use_global_device_ids=true, to_apply=%region_19.20 | all-reduce | flops 8 | bytes 64 | tf_op jit(solution)/shard_map/psum | solution.py:118
  401.0 6.5 %all-reduce.7 = (f32[]{:T(128)}, f32[]{:T(128)}, f32[]{:T(128)}, f32[]{:T(128)}, f32[]{:T(128)}, /*index=5*/f32[]{:T(128)}, f32[]{:T(128)}, f32[]{:T(128)}) all-reduce(f32[]{:T(128)} %get-tuple-element.480, f32[]{:T(128)} %get-tuple-element.481, f32[]{:T(128)} %get-tuple-element.482, ...), channel_id=1, replica_groups=mesh['layer'=8,'split'=4] {'split'}, use_global_device_ids=true, to_apply=%region_20.21 | all-reduce | flops 8 | bytes 64 | tf_op jit(solution)/shard_map/psum | solution.py:118
  (153 shorter events, 129.5 us)
Async XLA Ops:
  7.2 37.6 %all-gather.2.cloned.1.call-start = ((), (), s32[]{:S(2)}) async-start(), calls=%async_computation.2 | async-start | bytes 5242880 | tf_op jit(solution)/shard_map/all_gather | solution.py:86
  9.7 13.6 %all-to-all-start = ((f32[4,128,128]{1,0,2:T(4,128)}), f32[4,128,128]{1,0,2:T(4,128)S(1)}, u32[]{:S(2)}, u32[]{:S(2)}) async-start(f32[4,128,128]{1,0,2:T(4,128)} %copy.44), calls=%async_computation | async-start | bytes 524288 | tf_op jit(solution)/shard_map/all_to_all | solution.py:87
  14.7 326.8 %collective-permute-start.6 = (f32[1,128,128]{1,2,0:T(8,128)S(1)}, f32[1,128,128]{1,2,0:T(8,128)S(1)}, u32[]{:S(2)}, u32[]{:S(2)}) collective-permute-start(f32[1,128,128]{1,2,0:T(8,128)S(1)} %get-tuple-element.515), channel_id=1, source_target_pairs={{4,0},{8,4},{12,8},{16,12},{20,16},{24,20},{28,24},{5,1},{9,5},{13... | collective-permute-start | bytes 196616 | tf_op jit(solution)/shard_map/ppermute | solution.py:15
  18.0 323.5 %collective-permute-start.7 = (f32[1,128,128]{1,2,0:T(8,128)S(1)}, f32[1,128,128]{1,2,0:T(8,128)S(1)}, u32[]{:S(2)}, u32[]{:S(2)}) collective-permute-start(f32[1,128,128]{1,2,0:T(8,128)S(1)} %get-tuple-element.514), channel_id=1, source_target_pairs={{0,4},{4,8},{8,12},{12,16},{16,20},{20,24},{24,28},{1,5},{5,9},{9,... | collective-permute-start | bytes 196616 | tf_op jit(solution)/shard_map/ppermute | solution.py:14
  45.5 7.0 %collective-permute-start.1 = (f32[512,32]{0,1:T(8,128)S(1)}, f32[512,32]{0,1:T(8,128)S(1)}, u32[]{:S(2)}, u32[]{:S(2)}) collective-permute-start(f32[512,32]{0,1:T(8,128)S(1)} %get-tuple-element.651), channel_id=1, source_target_pairs={{0,4},{4,8},{8,12},{12,16},{16,20},{20,24},{24,28},{1,5},{5,9},{9,... | collective-permute-start | bytes 196616 | tf_op jit(solution)/shard_map/while/body/eval_jaxpr/ppermute | solution.py:23
  53.3 24.6 %collective-permute-start.1 = (f32[512,32]{0,1:T(8,128)S(1)}, f32[512,32]{0,1:T(8,128)S(1)}, u32[]{:S(2)}, u32[]{:S(2)}) collective-permute-start(f32[512,32]{0,1:T(8,128)S(1)} %get-tuple-element.651), channel_id=1, source_target_pairs={{0,4},{4,8},{8,12},{12,16},{16,20},{20,24},{24,28},{1,5},{5,9},{9,... | collective-permute-start | bytes 196616 | tf_op jit(solution)/shard_map/while/body/eval_jaxpr/ppermute | solution.py:23
  89.6 7.1 %collective-permute-start.1 = (f32[512,32]{0,1:T(8,128)S(1)}, f32[512,32]{0,1:T(8,128)S(1)}, u32[]{:S(2)}, u32[]{:S(2)}) collective-permute-start(f32[512,32]{0,1:T(8,128)S(1)} %get-tuple-element.651), channel_id=1, source_target_pairs={{0,4},{4,8},{8,12},{12,16},{16,20},{20,24},{24,28},{1,5},{5,9},{9,... | collective-permute-start | bytes 196616 | tf_op jit(solution)/shard_map/while/body/eval_jaxpr/ppermute | solution.py:23
  97.4 13.9 %collective-permute-start.1 = (f32[512,32]{0,1:T(8,128)S(1)}, f32[512,32]{0,1:T(8,128)S(1)}, u32[]{:S(2)}, u32[]{:S(2)}) collective-permute-start(f32[512,32]{0,1:T(8,128)S(1)} %get-tuple-element.651), channel_id=1, source_target_pairs={{0,4},{4,8},{8,12},{12,16},{16,20},{20,24},{24,28},{1,5},{5,9},{9,... | collective-permute-start | bytes 196616 | tf_op jit(solution)/shard_map/while/body/eval_jaxpr/ppermute | solution.py:23
  112.0 7.0 %collective-permute-start.1 = (f32[512,32]{0,1:T(8,128)S(1)}, f32[512,32]{0,1:T(8,128)S(1)}, u32[]{:S(2)}, u32[]{:S(2)}) collective-permute-start(f32[512,32]{0,1:T(8,128)S(1)} %get-tuple-element.651), channel_id=1, source_target_pairs={{0,4},{4,8},{8,12},{12,16},{16,20},{20,24},{24,28},{1,5},{5,9},{9,... | collective-permute-start | bytes 196616 | tf_op jit(solution)/shard_map/while/body/eval_jaxpr/ppermute | solution.py:23
  119.8 14.8 %collective-permute-start.1 = (f32[512,32]{0,1:T(8,128)S(1)}, f32[512,32]{0,1:T(8,128)S(1)}, u32[]{:S(2)}, u32[]{:S(2)}) collective-permute-start(f32[512,32]{0,1:T(8,128)S(1)} %get-tuple-element.651), channel_id=1, source_target_pairs={{0,4},{4,8},{8,12},{12,16},{16,20},{20,24},{24,28},{1,5},{5,9},{9,... | collective-permute-start | bytes 196616 | tf_op jit(solution)/shard_map/while/body/eval_jaxpr/ppermute | solution.py:23
  135.3 7.0 %collective-permute-start.1 = (f32[512,32]{0,1:T(8,128)S(1)}, f32[512,32]{0,1:T(8,128)S(1)}, u32[]{:S(2)}, u32[]{:S(2)}) collective-permute-start(f32[512,32]{0,1:T(8,128)S(1)} %get-tuple-element.651), channel_id=1, source_target_pairs={{0,4},{4,8},{8,12},{12,16},{16,20},{20,24},{24,28},{1,5},{5,9},{9,... | collective-permute-start | bytes 196616 | tf_op jit(solution)/shard_map/while/body/eval_jaxpr/ppermute | solution.py:23
  143.1 13.9 %collective-permute-start.1 = (f32[512,32]{0,1:T(8,128)S(1)}, f32[512,32]{0,1:T(8,128)S(1)}, u32[]{:S(2)}, u32[]{:S(2)}) collective-permute-start(f32[512,32]{0,1:T(8,128)S(1)} %get-tuple-element.651), channel_id=1, source_target_pairs={{0,4},{4,8},{8,12},{12,16},{16,20},{20,24},{24,28},{1,5},{5,9},{9,... | collective-permute-start | bytes 196616 | tf_op jit(solution)/shard_map/while/body/eval_jaxpr/ppermute | solution.py:23
  157.7 7.4 %collective-permute-start = (f32[512,32]{0,1:T(8,128)S(1)}, f32[512,32]{0,1:T(8,128)S(1)}, u32[]{:S(2)}, u32[]{:S(2)}) collective-permute-start(f32[512,32]{0,1:T(8,128)S(1)} %get-tuple-element.659), channel_id=1, source_target_pairs={{4,0},{8,4},{12,8},{16,12},{20,16},{24,20},{28,24},{5,1},{9,5},{13... | collective-permute-start | bytes 196616 | tf_op jit(solution)/shard_map/while/body/eval_jaxpr/ppermute | solution.py:23
  165.9 15.7 %collective-permute-start = (f32[512,32]{0,1:T(8,128)S(1)}, f32[512,32]{0,1:T(8,128)S(1)}, u32[]{:S(2)}, u32[]{:S(2)}) collective-permute-start(f32[512,32]{0,1:T(8,128)S(1)} %get-tuple-element.659), channel_id=1, source_target_pairs={{4,0},{8,4},{12,8},{16,12},{20,16},{24,20},{28,24},{5,1},{9,5},{13... | collective-permute-start | bytes 196616 | tf_op jit(solution)/shard_map/while/body/eval_jaxpr/ppermute | solution.py:23
  182.4 7.0 %collective-permute-start = (f32[512,32]{0,1:T(8,128)S(1)}, f32[512,32]{0,1:T(8,128)S(1)}, u32[]{:S(2)}, u32[]{:S(2)}) collective-permute-start(f32[512,32]{0,1:T(8,128)S(1)} %get-tuple-element.659), channel_id=1, source_target_pairs={{4,0},{8,4},{12,8},{16,12},{20,16},{24,20},{28,24},{5,1},{9,5},{13... | collective-permute-start | bytes 196616 | tf_op jit(solution)/shard_map/while/body/eval_jaxpr/ppermute | solution.py:23
  190.1 14.0 %collective-permute-start = (f32[512,32]{0,1:T(8,128)S(1)}, f32[512,32]{0,1:T(8,128)S(1)}, u32[]{:S(2)}, u32[]{:S(2)}) collective-permute-start(f32[512,32]{0,1:T(8,128)S(1)} %get-tuple-element.659), channel_id=1, source_target_pairs={{4,0},{8,4},{12,8},{16,12},{20,16},{24,20},{28,24},{5,1},{9,5},{13... | collective-permute-start | bytes 196616 | tf_op jit(solution)/shard_map/while/body/eval_jaxpr/ppermute | solution.py:23
  204.8 64.4 %collective-permute-start = (f32[512,32]{0,1:T(8,128)S(1)}, f32[512,32]{0,1:T(8,128)S(1)}, u32[]{:S(2)}, u32[]{:S(2)}) collective-permute-start(f32[512,32]{0,1:T(8,128)S(1)} %get-tuple-element.659), channel_id=1, source_target_pairs={{4,0},{8,4},{12,8},{16,12},{20,16},{24,20},{28,24},{5,1},{9,5},{13... | collective-permute-start | bytes 196616 | tf_op jit(solution)/shard_map/while/body/eval_jaxpr/ppermute | solution.py:23
  281.7 6.2 %collective-permute-start = (f32[512,32]{0,1:T(8,128)S(1)}, f32[512,32]{0,1:T(8,128)S(1)}, u32[]{:S(2)}, u32[]{:S(2)}) collective-permute-start(f32[512,32]{0,1:T(8,128)S(1)} %get-tuple-element.659), channel_id=1, source_target_pairs={{4,0},{8,4},{12,8},{16,12},{20,16},{24,20},{28,24},{5,1},{9,5},{13... | collective-permute-start | bytes 196616 | tf_op jit(solution)/shard_map/while/body/eval_jaxpr/ppermute | solution.py:23
  288.5 16.4 %collective-permute-start = (f32[512,32]{0,1:T(8,128)S(1)}, f32[512,32]{0,1:T(8,128)S(1)}, u32[]{:S(2)}, u32[]{:S(2)}) collective-permute-start(f32[512,32]{0,1:T(8,128)S(1)} %get-tuple-element.659), channel_id=1, source_target_pairs={{4,0},{8,4},{12,8},{16,12},{20,16},{24,20},{28,24},{5,1},{9,5},{13... | collective-permute-start | bytes 196616 | tf_op jit(solution)/shard_map/while/body/eval_jaxpr/ppermute | solution.py:23
  305.7 7.0 %collective-permute-start = (f32[512,32]{0,1:T(8,128)S(1)}, f32[512,32]{0,1:T(8,128)S(1)}, u32[]{:S(2)}, u32[]{:S(2)}) collective-permute-start(f32[512,32]{0,1:T(8,128)S(1)} %get-tuple-element.659), channel_id=1, source_target_pairs={{4,0},{8,4},{12,8},{16,12},{20,16},{24,20},{28,24},{5,1},{9,5},{13... | collective-permute-start | bytes 196616 | tf_op jit(solution)/shard_map/while/body/eval_jaxpr/ppermute | solution.py:23
  314.5 9.4 %all-to-all-start.1 = ((f32[4,1,16384]{2,1,0:T(1,128)}), f32[4,1,16384]{2,1,0:T(1,128)S(1)}, u32[]{:S(2)}, u32[]{:S(2)}) async-start(f32[4,1,16384]{2,1,0:T(1,128)} %reshape.6), calls=%async_computation.1 | async-start | bytes 524288 | tf_op jit(solution)/shard_map/all_to_all | solution.py:103
  326.8 15.1 %collective-permute-start.2 = (f32[1,128,128]{1,2,0:T(8,128)S(1)}, f32[1,128,128]{1,2,0:T(8,128)S(1)}, u32[]{:S(2)}, u32[]{:S(2)}) collective-permute-start(f32[1,128,128]{1,2,0:T(8,128)S(1)} %bitcast.60), channel_id=1, source_target_pairs={{4,0},{8,4},{12,8},{16,12},{20,16},{24,20},{28,24},{5,1},{9,5},{13... | collective-permute-start | bytes 196616 | tf_op jit(solution)/shard_map/ppermute | solution.py:15
  339.5 7.1 %collective-permute-start.3 = (f32[1,128,128]{1,2,0:T(8,128)S(1)}, f32[1,128,128]{1,2,0:T(8,128)S(1)}, u32[]{:S(2)}, u32[]{:S(2)}) collective-permute-start(f32[1,128,128]{1,2,0:T(8,128)S(1)} %bitcast.61), channel_id=1, source_target_pairs={{0,4},{4,8},{8,12},{12,16},{16,20},{20,24},{24,28},{1,5},{5,9},{9,... | collective-permute-start | bytes 196616 | tf_op jit(solution)/shard_map/ppermute | solution.py:14
  346.8 7.2 %collective-permute-start.4 = (f32[6,1,128]{1,2,0:T(8,128)S(1)}, f32[6,1,128]{1,2,0:T(8,128)S(1)}, u32[]{:S(2)}, u32[]{:S(2)}) collective-permute-start(f32[6,1,128]{1,2,0:T(8,128)S(1)} %get-tuple-element.508), channel_id=1, source_target_pairs={{1,0},{2,1},{3,2},{5,4},{6,5},{7,6},{9,8},{10,9},{11,10},{13,12},{... | collective-permute-start | bytes 9224 | tf_op jit(solution)/shard_map/ppermute | solution.py:15
  348.7 9.1 %collective-permute-start.5 = (f32[6,1,128]{1,2,0:T(8,128)S(1)}, f32[6,1,128]{1,2,0:T(8,128)S(1)}, u32[]{:S(2)}, u32[]{:S(2)}) collective-permute-start(f32[6,1,128]{1,2,0:T(8,128)S(1)} %get-tuple-element.509), channel_id=1, source_target_pairs={{0,1},{1,2},{2,3},{4,5},{5,6},{6,7},{8,9},{9,10},{10,11},{12,13},{... | collective-permute-start | bytes 9224 | tf_op jit(solution)/shard_map/ppermute | solution.py:14
  358.1 10.4 %collective-permute-start.10 = (f32[1,128,128]{1,2,0:T(8,128)S(1)}, f32[1,128,128]{1,2,0:T(8,128)S(1)}, u32[]{:S(2)}, u32[]{:S(2)}) collective-permute-start(f32[1,128,128]{1,2,0:T(8,128)S(1)} %get-tuple-element.511), channel_id=1, source_target_pairs={{4,0},{8,4},{12,8},{16,12},{20,16},{24,20},{28,24},{5,1},{9,5},{13... | collective-permute-start | bytes 196616 | tf_op jit(solution)/shard_map/ppermute | solution.py:15
  361.5 7.1 %collective-permute-start.11 = (f32[1,128,128]{1,2,0:T(8,128)S(1)}, f32[1,128,128]{1,2,0:T(8,128)S(1)}, u32[]{:S(2)}, u32[]{:S(2)}) collective-permute-start(f32[1,128,128]{1,2,0:T(8,128)S(1)} %get-tuple-element.510), channel_id=1, source_target_pairs={{0,4},{4,8},{8,12},{12,16},{16,20},{20,24},{24,28},{1,5},{5,9},{9,... | collective-permute-start | bytes 196616 | tf_op jit(solution)/shard_map/ppermute | solution.py:14
  364.1 9.7 %collective-permute-start.8 = (f32[6,1,128]{1,2,0:T(8,128)S(1)}, f32[6,1,128]{1,2,0:T(8,128)S(1)}, u32[]{:S(2)}, u32[]{:S(2)}) collective-permute-start(f32[6,1,128]{1,2,0:T(8,128)S(1)} %get-tuple-element.506), channel_id=1, source_target_pairs={{1,0},{2,1},{3,2},{5,4},{6,5},{7,6},{9,8},{10,9},{11,10},{13,12},{... | collective-permute-start | bytes 9224 | tf_op jit(solution)/shard_map/ppermute | solution.py:15
  366.1 9.1 %collective-permute-start.9 = (f32[6,1,128]{1,2,0:T(8,128)S(1)}, f32[6,1,128]{1,2,0:T(8,128)S(1)}, u32[]{:S(2)}, u32[]{:S(2)}) collective-permute-start(f32[6,1,128]{1,2,0:T(8,128)S(1)} %get-tuple-element.507), channel_id=1, source_target_pairs={{0,1},{1,2},{2,3},{4,5},{5,6},{6,7},{8,9},{9,10},{10,11},{12,13},{... | collective-permute-start | bytes 9224 | tf_op jit(solution)/shard_map/ppermute | solution.py:14
  368.8 8.4 %collective-permute-start.12 = (f32[6,1,128]{1,2,0:T(8,128)S(1)}, f32[6,1,128]{1,2,0:T(8,128)S(1)}, u32[]{:S(2)}, u32[]{:S(2)}) collective-permute-start(f32[6,1,128]{1,2,0:T(8,128)S(1)} %get-tuple-element.504), channel_id=1, source_target_pairs={{1,0},{2,1},{3,2},{5,4},{6,5},{7,6},{9,8},{10,9},{11,10},{13,12},{... | collective-permute-start | bytes 9224 | tf_op jit(solution)/shard_map/ppermute | solution.py:15
  371.9 9.1 %collective-permute-start.13 = (f32[6,1,128]{1,2,0:T(8,128)S(1)}, f32[6,1,128]{1,2,0:T(8,128)S(1)}, u32[]{:S(2)}, u32[]{:S(2)}) collective-permute-start(f32[6,1,128]{1,2,0:T(8,128)S(1)} %get-tuple-element.505), channel_id=1, source_target_pairs={{0,1},{1,2},{2,3},{4,5},{5,6},{6,7},{8,9},{9,10},{10,11},{12,13},{... | collective-permute-start | bytes 9224 | tf_op jit(solution)/shard_map/ppermute | solution.py:14
Sparse Core Ops, SparseCore 0:
  9.5 35.1 all-gather.1
